TPU v7x, 16 devices: a 4x2x1 block of a 4x4x8 slice. The times are simulated.
16 devices in a mesh: dp: 2 (over y, z), tp: 8 (over x, core).
Axes of the slice: x: 4, y: 2, z: 1, core: 2. Of those that a mesh axis runs over, the one named last changes fastest.
The devices are a block of a 4x4x8 slice.
Arguments:
- hidden: bfloat16 [32768, 1280], P(('dp', 'tp')), parts along dimension 0
- ln_gain: float32 [1280], replicated
- ln_bias: float32 [1280], replicated
- embed: bfloat16 [16384, 1280], P('tp')
- targets: int32 [32768], P(('dp', 'tp')), parts along dimension 0
- loss_mask: int32 [32768], P(('dp', 'tp')), parts along dimension 0
Outputs:
- output 1: float32 [32768], P(('dp', 'tp')), parts along dimension 0
- output 2: float32 [2], P('dp'), parts along dimension 0
- output 3: bfloat16 [32768, 1280], P(('dp', 'tp')), parts along dimension 0
- output 4: float32 [32768, 1280], P(('dp', 'tp')), parts along dimension 0
- output 5: float32 [2560], P('dp'), parts along dimension 0
- output 6: float32 [2560], P('dp'), parts along dimension 0
There are 2 independent parts. A program takes and returns all parts, laid end to end along the dimension named above; an argument that names none is the same for every part.
All inputs are finite; a program needn't handle non-finite values.
Results may differ from a plain program's by a relative error of at most 0.001.
Values are sent between devices in bfloat16 or wider.
A program may use at most 768 MiB of HBM per device.

v0:
```python
import jax
import jax.numpy as jnp
from jax import lax
from jax.sharding import PartitionSpec as P

LN_EPS = 1e-5


def layer_norm(hidden, ln_gain, ln_bias):
    h_f32 = hidden.astype(jnp.float32)
    centred = h_f32 - jnp.mean(h_f32, axis=-1, keepdims=True)
    inv_std = lax.rsqrt(jnp.mean(centred * centred, axis=-1, keepdims=True) + LN_EPS)
    x_hat = centred * inv_std
    return x_hat, inv_std, (x_hat * ln_gain + ln_bias).astype(jnp.bfloat16)


def norm_backward(d_normed, x_hat, inv_std, ln_gain):
    value_a6 = d_normed * ln_gain
    centre_term = jnp.mean(value_a6, axis=-1, keepdims=True)
    proj_term = jnp.mean(value_a6 * x_hat, axis=-1, keepdims=True)
    return (inv_std * (value_a6 - centre_term - x_hat * proj_term)).astype(jnp.bfloat16)


def solution(mesh):
    group = mesh.shape['tp']

    def body(hidden, ln_gain, ln_bias, embed, targets, loss_mask):
        tokens = hidden.shape[0]
        shard_vocab = embed.shape[0]
        rank = lax.axis_index('tp')
        x_hat, inv_std, normed = layer_norm(hidden, ln_gain, ln_bias)
        gathered = lax.all_gather(normed, 'tp', tiled=True)
        all_targets = lax.all_gather(targets, 'tp', tiled=True)
        all_weights = lax.all_gather(loss_mask, 'tp', tiled=True).astype(jnp.float32)
        count = lax.psum(jnp.sum(loss_mask.astype(jnp.float32)), 'tp')
        logits = jnp.einsum('sd,vd->sv', gathered, embed, preferred_element_type=jnp.float32)
        vocab_ids = rank * shard_vocab + lax.broadcasted_iota(jnp.int32, (1, shard_vocab), 1)
        onehot = vocab_ids == all_targets[:, None]
        local_max = jnp.max(logits, axis=-1)
        local_sum = jnp.sum(jnp.exp(logits - local_max[:, None]), axis=-1)
        local_target = jnp.sum(jnp.where(onehot, logits, 0.0), axis=-1)
        global_max = lax.pmax(local_max, 'tp')
        combined = lax.psum(jnp.stack([local_sum * jnp.exp(local_max - global_max), local_target]), 'tp')
        log_norm = global_max + jnp.log(combined[0])
        all_loss = (log_norm - combined[1]) * all_weights
        mean_loss = jnp.sum(all_loss) / count
        d_logits = ((jnp.exp(logits - log_norm[:, None]) - onehot.astype(jnp.float32)) * (all_weights / count)[:, None]).astype(jnp.bfloat16)
        d_embed = jnp.einsum('sv,sd->vd', d_logits, gathered, preferred_element_type=jnp.float32)
        d_part = jnp.einsum('sv,vd->sd', d_logits, embed, preferred_element_type=jnp.float32)
        d_normed = lax.psum_scatter(d_part, 'tp', scatter_dimension=0, tiled=True)
        norm_grads = lax.psum(jnp.stack([jnp.sum(d_normed * x_hat, axis=0), jnp.sum(d_normed, axis=0)]), 'tp')
        d_hidden = norm_backward(d_normed, x_hat, inv_std, ln_gain)
        own_loss = all_loss.reshape(group, tokens)[rank]
        return own_loss, mean_loss.reshape(1), d_hidden, d_embed, norm_grads[0], norm_grads[1]

    token_rows = P(('dp', 'tp'))
    token_mat = P(('dp', 'tp'), None)
    return jax.shard_map(body, mesh=mesh, in_specs=(token_mat, P(), P(), P('tp', None), token_rows, token_rows), out_specs=(token_rows, P('dp'), token_mat, token_mat, P('dp'), P('dp')), check_vma=False)
```

profile of v0, /device:TPU:112, one launch (start us, length us, event | category | flops | bytes accessed | tf_op | source)
XLA Modules:
  0.0 1035.0 jit_solution(11811916394017566745)
XLA Ops:
  7.2 0.0 copy-start.12
  7.2 0.0 copy-start.8
  7.2 0.1 all-gather.2.cloned.1.call-start
  7.3 0.0 copy-start
  7.3 3.4 convert_reduce_fusion
  10.7 0.0 copy-start.4
  10.7 0.0 copy-start.13
  10.7 4.0 fusion.17
  14.7 0.0 copy-done.4
  14.7 0.0 copy-start.6
  14.7 0.6 copy-done.6
  15.3 0.0 copy-done.12
  15.3 0.0 copy-done.8
  15.3 4.0 fusion.11
  19.3 0.1 all-gather.2.cloned.1.call-update
  19.4 0.1 all-reduce.4.cloned.1.call-start
  19.4 0.0 copy-done.13
  19.4 25.0 %all_gather.10 = s32[16384]{0:T(1024)} all-gather(s32[2048]{0:T(1024)S(1)} %copy-done.13), channel_id=1, replica_groups=mesh['dp'=2,'tp'=8] {'tp'}, dimensions={0}, use_global_device_ids=true | all-gather | bytes 73728 | tf_op jit(solution)/shard_map/all_gather | solution.py:33
  44.4 0.6 iota_add_fusion
  45.0 166.8 %all-gather.2.cloned.1.call-done = bf16[16384,1280]{1,0:T(8,128)(2,1)} async-done(((bf16[2048,1280]{1,0:T(8,128)(2,1)}), bf16[16384,1280]{1,0:T(8,128)(2,1)}) %all-gather.2.cloned.1.call-update) | async-done | bytes 41943056 | tf_op jit(solution)/shard_map/all_gather | solution.py:32
  211.8 99.5 %fusion.19 = (f32[16384]{0:T(1024)}, f32[16384,2048]{0,1:T(8,128)}) fusion(bf16[16384,1280]{1,0:T(8,128)(2,1)} %all-gather.2.cloned.1.call-done, bf16[2048,1280]{1,0:T(8,128)(2,1)} %param.9), kind=kOutput, calls=%fused_computation.40 | convolution fusion | flops 85932883968 | bytes 181469184 | tf_op jit(solution)/shard_map/sd,vd->sv/dot_general | solution.py:36
  311.3 0.1 all-reduce.4.cloned.1.call-update
  311.3 0.2 all-reduce.6.cloned.1.call-start
  311.6 0.0 copy-start.2
  311.6 0.0 copy-start.11
  311.6 45.4 %exponential_reduce_fusion = (f32[16384]{0:T(1024)S(1)}, f32[16384]{0:T(1024)S(1)}) fusion(f32[16384,2048]{0,1:T(8,128)} %get-tuple-element.21, f32[16384]{0:T(1024)} %get-tuple-element.20, s32[16384]{0:T(1024)S(1)} %copy-done.1, s32[2048]{0:T(1024)S(1)} %copy-done.10), kind=kLoop, calls=%fused_computation.6 | loop fusion | flops 167739392 | bytes 134488064 | tf_op jit(solution)/shard_map/reduce_sum | solution.py:40
  357.1 5.3 all-reduce.4.cloned.1.call-done
  362.4 0.9 exponential_multiply_fusion
  363.2 0.8 pad_maximum_fusion
  364.0 0.1 all-reduce.6.cloned.1.call-update
  364.1 0.1 reduce-scatter.4.cloned.1.call-start
  364.2 0.6 convert_reduce_fusion.1
  364.8 13.6 %psum.22 = f32[]{:T(128)} all-reduce(f32[]{:T(128)} %convert_reduce_fusion.1), channel_id=1, replica_groups=mesh['dp'=2,'tp'=8] {'tp'}, use_global_device_ids=true, to_apply=%region_9.10 | all-reduce | flops 1 | bytes 8 | tf_op jit(solution)/shard_map/psum | solution.py:35
  378.4 20.7 %all_gather.11 = s32[16384]{0:T(1024)S(1)} all-gather(s32[2048]{0:T(1024)S(1)} %copy-done.11), channel_id=1, replica_groups=mesh['dp'=2,'tp'=8] {'tp'}, dimensions={0}, use_global_device_ids=true | all-gather | bytes 73728 | tf_op jit(solution)/shard_map/all_gather | solution.py:34
  399.1 16.9 %all-reduce.6.cloned.1.call-done = f32[2,16384]{1,0:T(2,128)} async-done(((f32[2,16384]{1,0:T(2,128)}), f32[2,16384]{1,0:T(2,128)}) %all-reduce.6.cloned.1.call-update) | async-done | bytes 131088 | tf_op jit(solution)/shard_map/psum | solution.py:43
  416.0 1.1 slice_log_fusion
  417.1 2.7 fusion.18
  419.8 64.5 %fusion.3 = bf16[16384,2048]{0,1:T(8,128)(2,1)} fusion(f32[16384,2048]{0,1:T(8,128)} %get-tuple-element.21, f32[16384]{0:T(1024)S(1)} %get-tuple-element.19, f32[16384]{0:T(1024)S(1)} %get-tuple-element.16, s32[16384]{0:T(1024)S(1)} %copy-done.1, s32[2048]{0:T(1024)S(1)} %copy-done.10), kind=kLoop, calls=%fused_computation.5 | loop fusion | flops 201326592 | bytes 201531392 | tf_op jit(solution)/shard_map/convert_element_type | solution.py:47
  484.4 99.3 %fusion.20 = f32[16384,1280]{1,0:T(8,128)} fusion(bf16[16384,2048]{0,1:T(8,128)(2,1)} %fusion.3, bf16[2048,1280]{1,0:T(8,128)(2,1)} %param.9), kind=kOutput, calls=%fused_computation.41 | convolution fusion | flops 85899345920 | bytes 156237824 | tf_op jit(solution)/shard_map/sv,vd->sd/dot_general | solution.py:49
  583.6 0.1 reduce-scatter.4.cloned.1.call-update
  583.7 0.8 copy-done.3
  585.8 0.6 constant_dynamic-slice_fusion
  586.4 98.4 %fusion.21 = f32[2048,1280]{1,0:T(8,128)} fusion(bf16[16384,2048]{0,1:T(8,128)(2,1)} %fusion.3, bf16[16384,1280]{1,0:T(8,128)(2,1)} %all-gather.2.cloned.1.call-done), kind=kOutput, calls=%fused_computation.42 | convolution fusion | flops 85899345920 | bytes 119537664 | tf_op jit(solution)/shard_map/sv,sd->vd/dot_general | solution.py:48
  684.9 300.2 %reduce-scatter.4.cloned.1.call-done = f32[2048,1280]{1,0:T(8,128)} async-done(((f32[16384,1280]{1,0:T(8,128)}), f32[2048,1280]{1,0:T(8,128)}) %reduce-scatter.4.cloned.1.call-update) | async-done | bytes 10485776
  985.1 7.9 fusion.16
  993.1 23.6 %psum.23 = f32[2,1280]{1,0:T(2,128)S(1)} all-reduce(f32[2,1280]{1,0:T(2,128)S(1)} %pad_maximum_fusion.1), channel_id=1, replica_groups=mesh['dp'=2,'tp'=8] {'tp'}, use_global_device_ids=true, to_apply=%region_15.16 | all-reduce | flops 2560 | bytes 20480 | tf_op jit(solution)/shard_map/psum | solution.py:51
  1016.7 0.6 slice_reduce_fusion
  1017.3 9.7 fusion.15
  (21 shorter events, 0.1 us)
Async XLA Ops:
  7.2 8.2 copy-start.12
  7.2 8.1 copy-start.8
  7.2 204.6 %all-gather.2.cloned.1.call-start = ((), (), s32[]{:S(2)}) async-start(), calls=%async_computation.1 | async-start | bytes 47185920 | tf_op jit(solution)/shard_map/all_gather | solution.py:32
  7.3 8.1 copy-start
  10.7 4.0 copy-start.4
  10.7 8.7 copy-start.13
  14.7 0.6 copy-start.6
  19.4 343.0 %all-reduce.4.cloned.1.call-start = ((), (), s32[]{:S(2)}) async-start(), calls=%async_computation.2 | async-start | bytes 131072 | tf_op jit(solution)/shard_map/pmax | solution.py:42
  211.8 99.8 %copy-start.1 = (s32[16384]{0:T(1024)S(1)}, s32[16384]{0:T(1024)}, u32[]{:S(2)}) copy-start(s32[16384]{0:T(1024)} %all_gather.10) | copy-start | bytes 196612
  211.8 99.8 %copy-start.10 = (s32[2048]{0:T(1024)S(1)}, s32[2048]{0:T(1024)}, u32[]{:S(2)}) copy-start(s32[2048]{0:T(1024)} %iota_add_fusion) | copy-start | bytes 24580
  311.3 104.6 %all-reduce.6.cloned.1.call-start = ((), (), s32[]{:S(2)}) async-start(), calls=%async_computation.3 | async-start | bytes 262144 | tf_op jit(solution)/shard_map/psum | solution.py:43
  311.6 50.8 %copy-start.2 = (f32[16384]{0:T(1024)S(1)}, f32[16384]{0:T(1024)}, u32[]{:S(2)}) copy-start(f32[16384]{0:T(1024)} %get-tuple-element.20) | copy-start | bytes 196612
  311.6 52.5 %copy-start.11 = (s32[2048]{0:T(1024)S(1)}, s32[2048]{0:T(1024)}, u32[]{:S(2)}) copy-start(s32[2048]{0:T(1024)} %param.11) | copy-start | bytes 24580
  364.1 621.0 %reduce-scatter.4.cloned.1.call-start = ((), (), s32[]{:S(2)}) async-start(), calls=%async_computation.4 | async-start | bytes 94371840
  583.6 0.8 copy-start.3
  586.4 398.7 %copy-start.5 = (f32[2048]{0:T(1024)S(1)}, f32[2048]{0:T(1024)}, u32[]{:S(2)}) copy-start(f32[2048]{0:T(1024)} %copy-done.4) | copy-start | bytes 24580
  586.4 398.7 %copy-start.7 = (f32[2048]{0:T(1024)S(1)}, f32[2048]{0:T(1024)}, u32[]{:S(2)}) copy-start(f32[2048]{0:T(1024)} %copy-done.6) | copy-start | bytes 24580
  586.4 398.7 %copy-start.9 = (f32[1280]{0:T(1024)S(1)}, f32[1280]{0:T(1024)}, u32[]{:S(2)}) copy-start(f32[1280]{0:T(1024)} %param.7) | copy-start | bytes 15364
Sparse Core Ops, SparseCore 0:
  19.5 192.2 all-gather.1
  311.5 50.8 all-reduce.3
  365.3 50.6 all-reduce.5
  583.8 401.2 reduce-scatter.3
where the time goes:
time: 1040 us; the launch traced here: 1030 us
  waiting for transfers between devices  489 us (47%)
  matrix products  297 us (29%)
  other arithmetic  145 us (14%)
  blocking collectives  82.9 us (8%)
  between operations  16.7 us (2%)
    unnamed x5, waiting for transfers between devices  300 us
    all_gather x1, waiting for transfers between devices, body(): gathered = lax.all_gather(normed, 'tp', tiled=True)  167 us
    dot_general x1, matrix products, body(): jnp.einsum('sd,vd->sv', gathered, embed, preferred_element_type=jnp.float32)  99.5 us
    dot_general x1, matrix products, body(): jnp.einsum('sv,vd->sd', d_logits, embed, preferred_element_type=jnp.float32)  99.3 us
    dot_general x1, matrix products, body(): jnp.einsum('sv,sd->vd', d_logits, gathered, preferred_element_type=jnp.fl...  98.4 us
    convert_element_type x1, other arithmetic, body(): ((jnp.exp(logits - log_norm[:, None]) - onehot.astype(jnp.float32)) * (al...  64.5 us
    reduce_sum x1, other arithmetic, body(): local_sum = jnp.sum(jnp.exp(logits - local_max[:, None]), axis=-1)  45.4 us
    all_gather x1, blocking collectives, body(): all_targets = lax.all_gather(targets, 'tp', tiled=True)  25 us
  transfers between devices with their start and end apart: 4, of which 4 were waited for; matrix products, arithmetic and copies ran while one was open for 14% of the time, Pallas kernels for 0%

commit v1 on v0

v1 whole, which is shorter than its diff:
```python
import functools

import jax
import jax.numpy as jnp
from jax import lax
from jax.experimental import pallas as pl
from jax.experimental.pallas import tpu as pltpu
from jax.sharding import PartitionSpec as P


LN_EPS = 1e-5
F32 = jnp.float32
BF16 = jnp.bfloat16
LANES = 128
VMEM_LIMIT = 62 << 20
PIECES = 4
TOKEN_CHUNKS = 2
MIN_GATHER = 1 << 20


def params():
    return pltpu.CompilerParams(vmem_limit_bytes=VMEM_LIMIT, dimension_semantics=('arbitrary',))


def cost(matmuls, rows, cols, depth, extra):
    return pl.CostEstimate(flops=2 * matmuls * rows * cols * depth, bytes_accessed=extra, transcendentals=rows * cols)


NEAR, FAR, OPPOSITE = -1, 1, 2
FOREIGN = [(NEAR, 0), (FAR, 0), (NEAR, 1), (FAR, 1), (FAR, 2), (NEAR, 2), (OPPOSITE, 0), (FAR, 3), (NEAR, 3), (OPPOSITE, 1), (OPPOSITE, 2), (OPPOSITE, 3)]
LINK = {item: item[1] for item in FOREIGN if item[0] == NEAR}
LINK.update({(FAR, 0): 4, (FAR, 1): 5, (OPPOSITE, 0): 6, (OPPOSITE, 1): 7, (FAR, 2): 8, (FAR, 3): 9, (OPPOSITE, 2): 10, (OPPOSITE, 3): 11})
SIBLING = 12
COPIES = SIBLING + PIECES + len(FOREIGN)
CHIPS = 4


def step_order():
    order = [(0, core, n) for core in (0, 1) for n in range(PIECES)]
    for a in range(0, len(FOREIGN), 2):
        pair = FOREIGN[a:a + 2]
        cores = [(0, pair[0]), (0, pair[1]), (1, pair[0]), (1, pair[1])]
        if a + 2 == len(FOREIGN):
            cores = [cores[0], cores[2], cores[1], cores[3]]
        order += [(chip, core, n) for core, (chip, n) in cores]
    return order


ORDER = step_order()


def place(chip, core, n):
    odd = lax.rem(lax.axis_index('dp'), 2)
    me = lax.axis_index('tp')
    sign = 1 - 2 * odd
    shard = lax.rem(me // 2 + chip * sign + CHIPS, CHIPS) * 2 + lax.rem(lax.rem(me, 2) + core, 2)
    return shard, lax.rem(odd * (PIECES // 2) + n, PIECES)


def logits_body(rows, h_ref, gain_ref, bias_ref, own_ref, *refs):
    x_refs = refs[:TOKEN_CHUNKS]
    lse_ref, norms_ref, all_ref, z_ref, e_buf, z_buf, m_ref, s_ref, e_sem, o_sem, z_sem, send_sem, recv_sem = refs[TOKEN_CHUNKS:]
    i = pl.program_id(0)
    steps = len(ORDER)
    tile = e_buf.shape[1]
    shard_rows = own_ref.shape[0]
    slot = lax.rem(i, 2)
    dp, me = lax.axis_index('dp'), lax.axis_index('tp')
    odd = lax.rem(dp, 2)
    sign = 1 - 2 * odd
    chip, core = me // 2, lax.rem(me, 2)
    targets = {
        'ahead': (dp, lax.rem(chip + sign + CHIPS, CHIPS) * 2 + core),
        'back': (dp, lax.rem(chip - sign + CHIPS, CHIPS) * 2 + core),
        'sibling': (dp, chip * 2 + 1 - core),
        'across': (dp + sign, me),
    }

    def rows_of(entry):
        shard, piece = place(*entry)
        return pl.ds(pl.multiple_of(shard * shard_rows + piece * tile, tile), tile)

    def own_rows(n):
        return pl.ds(pl.multiple_of(place(0, 0, n)[1] * tile, tile), tile)

    def remote(to, number, entry, own=False):
        at = rows_of(entry)
        source = own_ref.at[own_rows(entry[2]), :] if own else all_ref.at[at, :]
        return pltpu.make_async_remote_copy(source, all_ref.at[at, :], send_sem.at[number], recv_sem.at[number], device_id=targets[to], device_id_type=pl.DeviceIdType.MESH)

    def arrived(number):
        remote('sibling', number, ORDER[0]).wait_recv()

    def load(step):
        entry = ORDER[step]
        source = own_ref.at[own_rows(entry[2]), :] if step < PIECES else all_ref.at[rows_of(entry), :]
        pltpu.make_async_copy(source, e_buf.at[step % 2], e_sem.at[step % 2]).start()

    def keep(step):
        return pltpu.make_async_copy(e_buf.at[step % 2], all_ref.at[rows_of(ORDER[step]), :], o_sem.at[step % 2])

    def receive(step):
        chip_of, core_of, n = ORDER[step]
        if chip_of == 0 and core_of == 0:
            return
        if chip_of == 0:
            arrived(SIBLING + n)
            return
        number = FOREIGN.index((chip_of, n))
        if core_of == 1:
            arrived(SIBLING + PIECES + number)
            return
        arrived(LINK[chip_of, n])
        entry = ORDER[step]
        remote('sibling', SIBLING + PIECES + number, entry).start()
        if n < 2:
            if chip_of == FAR:
                remote('back', LINK[OPPOSITE, n], entry).start()
            elif chip_of == NEAR:
                remote('across', LINK[FAR, n + 2], entry).start()
            else:
                remote('across', LINK[OPPOSITE, n + 2], entry).start()

    @pl.when(i == 0)
    def _():
        barrier = pltpu.get_barrier_semaphore()
        for to in targets.values():
            pl.semaphore_signal(barrier, inc=1, device_id=to, device_id_type=pl.DeviceIdType.MESH)
        pl.semaphore_wait(barrier, len(targets))
        for n in range(PIECES):
            remote('ahead', LINK[NEAR, n], (0, 0, n), own=True).start()
            if n < 2:
                remote('back', LINK[FAR, n], (0, 0, n), own=True).start()
            remote('sibling', SIBLING + n, (0, 0, n), own=True).start()
        load(0)

        for c, x_ref in enumerate(x_refs):
            @pl.loop(0, x_ref.shape[0] // rows)
            def _(a, c=c, x_ref=x_ref):
                h = h_ref[pl.ds(pl.multiple_of(c * x_ref.shape[0] + a * rows, rows), rows), :].astype(F32)
                centred = h - jnp.mean(h, axis=-1, keepdims=True)
                inv_std = lax.rsqrt(jnp.mean(centred * centred, axis=-1, keepdims=True) + LN_EPS)
                x_ref[pl.ds(pl.multiple_of(a * rows, rows), rows), :] = (centred * inv_std * gain_ref[...] + bias_ref[...]).astype(BF16)
        m_ref[...] = jnp.full_like(m_ref, -jnp.inf)
        s_ref[...] = jnp.zeros_like(s_ref)

    pltpu.make_async_copy(own_ref.at[pl.ds(0, tile), :], e_buf.at[slot], e_sem.at[slot]).wait()
    for step in range(steps):
        @pl.when(i == step)
        def _(step=step):
            if step < PIECES:
                keep(step).start()
            if 1 <= step <= PIECES:
                keep(step - 1).wait()
            if step + 1 < steps:
                receive(step + 1)
                load(step + 1)

    def written(step):
        return pltpu.make_async_copy(z_buf.at[lax.rem(step, 2)], z_ref.at[:, pl.ds(pl.multiple_of(step * tile, tile), tile)], z_sem.at[lax.rem(step, 2)])

    @pl.when(i >= 2)
    def _():
        written(i - 2).wait()

    held = x_refs[0].shape[0]
    for r in range(0, h_ref.shape[0], rows):
        part = slice(r, r + rows)
        z = lax.dot_general(x_refs[r // held][r % held:r % held + rows, :], e_buf[slot], (((1,), (1,)), ((), ())), preferred_element_type=F32)
        z_buf[slot, part, :] = z
        m_old = m_ref[part, :]
        m_new = m_old
        for g in range(0, tile, LANES):
            m_new = jnp.maximum(m_new, z[:, g:g + LANES])
        total = s_ref[part, :] * jnp.exp(m_old - m_new)
        for g in range(0, tile, LANES):
            total = total + jnp.exp(z[:, g:g + LANES] - m_new)
        m_ref[part, :] = m_new
        s_ref[part, :] = total
    written(i).start()

    @pl.when(i == steps - 1)
    def _():
        m = m_ref[...]
        top = jnp.max(m, axis=-1, keepdims=True)
        total = jnp.sum(s_ref[...] * jnp.exp(m - top), axis=-1, keepdims=True)
        lse = jnp.broadcast_to(top + jnp.log(total), lse_ref.shape)
        lse_ref[...] = lse
        norms_ref[...] = lse.T[:norms_ref.shape[0]]
        written(i - 1).wait()
        written(i).wait()
        for number in range(COPIES):
            remote('sibling', number, ORDER[0]).wait_send()


def logits_call(hidden, gain, bias, embed, vocab, copies, rows=256):
    tokens, dim = hidden.shape
    tile = embed.shape[0] // PIECES
    whole = lambda shape: pl.BlockSpec(shape, lambda i: (0, 0), pipeline_mode=pl.Buffered(1))
    fixed = lambda shape: pl.BlockSpec(shape, lambda i: (0, 0))
    hbm = pl.BlockSpec(memory_space=pl.ANY)
    return pl.pallas_call(
        functools.partial(logits_body, rows),
        grid=(len(ORDER),),
        in_specs=[whole((tokens, dim)), whole((1, dim)), whole((1, dim)), hbm],
        out_specs=[fixed((tokens // TOKEN_CHUNKS, dim))] * TOKEN_CHUNKS + [fixed((tokens, LANES)), fixed((copies, tokens)), hbm, hbm],
        out_shape=[jax.ShapeDtypeStruct((tokens // TOKEN_CHUNKS, dim), BF16)] * TOKEN_CHUNKS + [
            jax.ShapeDtypeStruct((tokens, LANES), F32),
            jax.ShapeDtypeStruct((copies, tokens), F32),
            jax.ShapeDtypeStruct((vocab, dim), BF16),
            jax.ShapeDtypeStruct((tokens, vocab), F32),
        ],
        scratch_shapes=[
            pltpu.VMEM((2, tile, dim), BF16),
            pltpu.VMEM((2, tokens, tile), F32),
            pltpu.VMEM((tokens, LANES), F32),
            pltpu.VMEM((tokens, LANES), F32),
            pltpu.SemaphoreType.DMA((2,)),
            pltpu.SemaphoreType.DMA((2,)),
            pltpu.SemaphoreType.DMA((2,)),
            pltpu.SemaphoreType.DMA((COPIES,)),
            pltpu.SemaphoreType.DMA((COPIES,)),
        ],
        compiler_params=pltpu.CompilerParams(vmem_limit_bytes=VMEM_LIMIT, dimension_semantics=('arbitrary',), collective_id=0, has_side_effects=True),
        cost_estimate=cost(1, tokens, vocab, dim, 4 * tokens * vocab),
        name='logits',
    )(hidden, gain.reshape(1, dim), bias.reshape(1, dim), embed)


def own_grad_body(rows, order_ref, z_ref, e_ref, h_ref, gain_ref, lse_ref, tgt_row, w_row, dh_ref, loss_ref, sums_ref, acc_ref, t_ref, tgt_ref, w_ref):
    i = pl.program_id(0)
    tokens, tile = z_ref.shape
    base = order_ref[i] * tile

    @pl.when(i == 0)
    def _():
        acc_ref[...] = jnp.zeros_like(acc_ref)
        t_ref[...] = jnp.zeros_like(t_ref)
        tgt_ref[...] = jnp.broadcast_to(tgt_row[...], (LANES, tokens)).T
        w_ref[...] = jnp.broadcast_to(w_row[...], (LANES, tokens)).T

    lane = lax.broadcasted_iota(jnp.int32, (rows, LANES), 1)
    for r in range(0, tokens, rows):
        part = slice(r, r + rows)
        lse, tgt, w = lse_ref[part, :], tgt_ref[part, :] - base, w_ref[part, :]
        picked = t_ref[part, :]
        pieces = []
        for g in range(0, tile, LANES):
            z = z_ref[part, g:g + LANES]
            hit = lane + g == tgt
            p = jnp.exp(z - lse)
            p = jnp.where(hit, p - 1.0, p) * w
            picked = picked + jnp.where(hit, z, 0.0)
            pieces.append(p.astype(BF16))
        t_ref[part, :] = picked
        acc_ref[part, :] += jnp.dot(jnp.concatenate(pieces, axis=1), e_ref[...], preferred_element_type=F32)

    @pl.when(i == pl.num_programs(0) - 1)
    def _():
        loss = lse_ref[...] - jnp.sum(t_ref[...], axis=-1, keepdims=True)
        loss = jnp.where(w_ref[...] > 0.0, loss, 0.0)
        loss_ref[...] = loss.T[:8]
        sums_ref[...] = jnp.zeros_like(sums_ref)
        sums_ref[2:3, 0:LANES] = jnp.sum(loss, axis=0, keepdims=True)

        @pl.loop(0, tokens // rows)
        def _(a):
            part = pl.ds(pl.multiple_of(a * rows, rows), rows)
            h = h_ref[part, :].astype(F32)
            centred = h - jnp.mean(h, axis=-1, keepdims=True)
            inv_std = lax.rsqrt(jnp.mean(centred * centred, axis=-1, keepdims=True) + LN_EPS)
            x_hat = centred * inv_std
            d = acc_ref[part, :]
            sums_ref[0:1, :] += jnp.sum(d * x_hat, axis=0, keepdims=True)
            sums_ref[1:2, :] += jnp.sum(d, axis=0, keepdims=True)
            g = d * gain_ref[...]
            centre_term = jnp.mean(g, axis=-1, keepdims=True)
            proj_term = jnp.mean(g * x_hat, axis=-1, keepdims=True)
            dh_ref[part, :] = (inv_std * (g - centre_term - x_hat * proj_term)).astype(BF16)


def own_grad_call(order, z, e, hidden, gain, lse, tgt, w, tile, copies, rows=256):
    tokens, vocab = z.shape
    dim = e.shape[1]
    once = lambda shape: pl.BlockSpec(shape, lambda i, order: (0, 0), pipeline_mode=pl.Buffered(1))
    fixed = lambda shape: pl.BlockSpec(shape, lambda i, order: (0, 0))
    return pl.pallas_call(
        functools.partial(own_grad_body, rows),
        grid_spec=pltpu.PrefetchScalarGridSpec(
            num_scalar_prefetch=1,
            grid=(vocab // tile,),
            in_specs=[
                pl.BlockSpec((tokens, tile), lambda i, order: (0, i)),
                pl.BlockSpec((tile, dim), lambda i, order: (order[i], 0)),
                once((tokens, dim)),
                once((1, dim)),
                once((tokens, LANES)),
                once((1, tokens)),
                once((1, tokens)),
            ],
            out_specs=[fixed((tokens, dim)), fixed((8, tokens)), fixed((copies, dim))],
            scratch_shapes=[
                pltpu.VMEM((tokens, dim), F32),
                pltpu.VMEM((tokens, LANES), F32),
                pltpu.VMEM((tokens, LANES), jnp.int32),
                pltpu.VMEM((tokens, LANES), F32),
            ],
        ),
        out_shape=[
            jax.ShapeDtypeStruct((tokens, dim), BF16),
            jax.ShapeDtypeStruct((8, tokens), F32),
            jax.ShapeDtypeStruct((copies, dim), F32),
        ],
        compiler_params=params(),
        cost_estimate=cost(1, tokens, vocab, dim, 4 * tokens * vocab),
        name='own_grad',
    )(order, z, e, hidden, gain.reshape(1, dim), lse, tgt, w)


def d_embed_body(rows, first_ref, count_ref, x_ref, e_ref, lse_ref, info_ref, *refs):
    o_ref = refs[-1]

    @pl.when(pl.program_id(0) == 0)
    def _():
        if len(refs) == 1:
            o_ref[...] = jnp.zeros_like(o_ref)
        else:
            pltpu.sync_copy(refs[0], o_ref)

    width = x_ref.shape[0]
    info = info_ref[0:1, :]
    lse, tgt, w = lse_ref[0:1, :], (info >> 1) - first_ref[0], (info & 1).astype(F32) / count_ref[0]
    row = lax.broadcasted_iota(jnp.int32, (rows, width), 0)
    for r in range(0, e_ref.shape[0], rows):
        z = lax.dot_general(e_ref[r:r + rows, :], x_ref[...], (((1,), (1,)), ((), ())), preferred_element_type=F32)
        p = jnp.exp(z - lse)
        p = jnp.where(row == tgt - r, p - 1.0, p) * w
        o_ref[r:r + rows, :] += jnp.dot(p.astype(BF16), x_ref[...], preferred_element_type=F32)


def d_embed_call(first, count, x, e, lse, info, before, chunk, tile, rows=256):
    tokens, dim = x.shape
    shard = e.shape[0]
    scalar = pl.BlockSpec(memory_space=pltpu.SMEM)
    stat = lambda v: pl.BlockSpec((v.shape[0] * tile // tokens, tile), lambda i: (i, chunk))
    in_specs = [scalar, scalar, pl.BlockSpec((tile, dim), lambda i: (i, 0)), pl.BlockSpec((shard, dim), lambda i: (0, 0)), stat(lse), stat(info)]
    operands = [first.reshape(1), count.reshape(1), x, e, lse, info]
    if before is not None:
        in_specs.append(pl.BlockSpec(memory_space=pl.ANY))
        operands.append(before)
    return pl.pallas_call(
        functools.partial(d_embed_body, rows),
        grid=(tokens // tile,),
        in_specs=in_specs,
        out_specs=pl.BlockSpec((shard, dim), lambda i: (0, 0)),
        out_shape=jax.ShapeDtypeStruct((shard, dim), F32),
        compiler_params=params(),
        cost_estimate=cost(2, tokens, shard, dim, 2 * tokens * dim + 8 * shard * dim),
        name='d_embed',
    )(*operands)


def solution(mesh):
    group = mesh.shape['tp']

    def whole(hidden, ln_gain, ln_bias, embed, targets, loss_mask):
        tokens, dim = hidden.shape
        shard = embed.shape[0]
        rank = lax.axis_index('tp')
        copies = lambda width: -(-MIN_GATHER // (4 * group * width))
        info = lax.all_gather(jnp.tile((targets * 2 + loss_mask).reshape(1, tokens), (copies(tokens), 1)), 'tp', tiled=True)
        count = jnp.sum((info.reshape(group, -1, tokens)[:, 0] & 1).astype(F32))

        outs = logits_call(hidden, ln_gain, ln_bias, embed, shard * group, copies(tokens))
        lse, norms, all_embed, z = outs[TOKEN_CHUNKS:]
        x_chunks = []
        for h in range(TOKEN_CHUNKS):
            x_chunks.append(lax.all_gather(outs[h], 'tp', tiled=True))
        norms = lax.all_gather(norms, 'tp', tiled=True)

        places = [place(*entry) for entry in ORDER]
        order = jnp.stack([shard_of * PIECES + n for shard_of, n in places])
        scale = loss_mask.astype(F32) / count
        extra = -(-copies(dim) // 8) * 8
        d_hidden, loss, sums = own_grad_call(order, z, all_embed, hidden, ln_gain, lse, targets.reshape(1, tokens), scale.reshape(1, tokens), shard // PIECES, extra)
        sums = jnp.sum(lax.all_gather(sums, 'tp', tiled=True).reshape(group, extra, dim)[:, :3], axis=0)
        mean_loss = jnp.sum(sums[2, :LANES]) / LANES / count

        d_embed = None
        for h in range(TOKEN_CHUNKS):
            d_embed = d_embed_call(rank * shard, count, x_chunks[h], embed, norms, info, d_embed, h, tokens // TOKEN_CHUNKS)
        return loss[0], mean_loss.reshape(1), d_hidden, d_embed, sums[0], sums[1]

    token_rows = P(('dp', 'tp'))
    token_mat = P(('dp', 'tp'), None)
    return jax.shard_map(whole, mesh=mesh, in_specs=(token_mat, P(), P(), P('tp', None), token_rows, token_rows), out_specs=(token_rows, P('dp'), token_mat, token_mat, P('dp'), P('dp')), check_vma=False)
```

time: 1040 us -> 671 us (0.65)
  Pallas kernels: 0 us -> 504 us
  waiting for transfers between devices: 489 us -> 138 us
  matrix products: 297 us -> 0 us
  other arithmetic: 145 us -> 5.33 us
  blocking collectives: 82.9 us -> 0 us
    pallas_call x0 -> x4, Pallas kernels: none -> 504 us  [the longest x2 202 us: d_embed_call(): pl.pallas_call(functools.partial(d_embed_body, rows), grid=(tokens // til...]
    unnamed x5, waiting for transfers between devices: 300 us -> 1.78 us
    dot_general x3 -> x0, matrix products: 297 us -> none  [the longest x1 99.5 us: body(): jnp.einsum('sd,vd->sv', gathered, embed, preferred_element_type=jnp.float32)]
    convert_element_type x3 -> x0, other arithmetic: 78.2 us -> none  [the longest x1 64.5 us: body(): ((jnp.exp(logits - log_norm[:, None]) - onehot.astype(jnp.float32)) * (al...]
    reduce_sum x6 -> x3, other arithmetic: 64.1 us -> 3.39 us  [the longest x1 1.79 us: whole(): count = jnp.sum((info.reshape(group, -1, tokens)[:, 0] & 1).astype(F32))]
    all_gather x2 -> x0, blocking collectives: 45.7 us -> none  [the longest x1 25 us: body(): all_targets = lax.all_gather(targets, 'tp', tiled=True)]
    psum x2 -> x0, blocking collectives: 37.2 us -> none  [the longest x1 23.6 us: body(): lax.psum(jnp.stack([jnp.sum(d_normed * x_hat, axis=0), jnp.sum(d_normed,...]
    all_gather x1 -> x5, waiting for transfers between devices: 167 us -> 136 us  [the longest x2 101 us: whole(): x_chunks.append(lax.all_gather(outs[h], 'tp', tiled=True))]
  transfers between devices with their start and end apart: 4 -> 5, of which waited for: 4 -> 4; matrix products, arithmetic and copies ran while one was open for 14% -> 1% of each run, Pallas kernels for 0% -> 41%
where the time goes in v1:
time: 671 us; the launch traced here: 670 us
  Pallas kernels  504 us (75%)
  waiting for transfers between devices  138 us (21%)
  between operations  16.3 us (2%)
    pallas_call x2, Pallas kernels, d_embed_call(): pl.pallas_call(functools.partial(d_embed_body, rows), grid=(tokens // til...  202 us
    pallas_call x1, Pallas kernels, logits_call(): pl.pallas_call(functools.partial(logits_body, rows), grid=(len(ORDER),),...  179 us
    pallas_call x1, Pallas kernels, own_grad_call(): pl.pallas_call(functools.partial(own_grad_body, rows), grid_spec=pltpu.Pr...  123 us
    all_gather x2, waiting for transfers between devices, whole(): x_chunks.append(lax.all_gather(outs[h], 'tp', tiled=True))  101 us
    all_gather x1, waiting for transfers between devices, whole(): norms = lax.all_gather(norms, 'tp', tiled=True)  17.4 us
    all_gather x1, waiting for transfers between devices, whole(): lax.all_gather(sums, 'tp', tiled=True).reshape(group, extra, dim)[:, :3]  17.3 us
  transfers between devices with their start and end apart: 5, of which 4 were waited for; matrix products, arithmetic and copies ran while one was open for 1% of the time, Pallas kernels for 41%

profile of v1, /device:TPU:112, one launch (start us, length us, event | category | flops | bytes accessed | tf_op | source)
XLA Modules:
  0.0 670.2 jit_solution(10178082024063170177)
XLA Ops:
  7.2 0.1 all-gather.6.cloned.1.call-start
  7.2 0.7 multiply_add_fusion
  8.0 0.7 tile.2
  8.6 0.1 all-gather.6.cloned.1.call-update
  8.7 0.1 all-gather.8.cloned.1.call-start
  8.8 1.3 reshape.48.gain_ref
  10.1 1.3 reshape.49.bias_ref
  11.4 0.0 copy-start
  11.4 178.7 %logits.1 = (bf16[1024,1280]{1,0:T(8,128)(2,1)}, bf16[1024,1280]{1,0:T(8,128)(2,1)}, f32[2048,128]{1,0:T(8,128)}, f32[16,2048]{1,0:T(8,128)}, bf16[16384,1280]{1,0:T(8,128)(2,1)}, /*index=5*/f32[2048,16384]{1,0:T(8,128)}) custom-call(bf16[2048,1280]{1,0:T(8,128)(2,1)} %h_ref.3, f32[1,1280]{1,0:T(1,128)} %reshape.48.gain_ref, f32[1,1280]{1,0:T(1,128)} %reshape.49.bias_ref, ...), custom_call_target="tpu_custom_call" | custom-call | flops 85899345920 | bytes 134217728 | tf_op jit(solution)/shard_map/logits/pallas_call | solution.py:202
  190.2 0.7 stack.131.order_ref
  190.8 0.0 all-gather.6.cloned.1.call-done.info_ref
  190.8 1.8 fusion.1
  192.6 0.0 copy-done
  192.6 1.2 convert_divide_fusion
  193.9 123.5 %own_grad.1 = (bf16[2048,1280]{1,0:T(8,128)(2,1)}, f32[8,2048]{1,0:T(8,128)}, f32[32,1280]{1,0:T(8,128)}) custom-call(s32[32]{0:T(128)} %stack.131.order_ref, f32[2048,16384]{1,0:T(8,128)} %get-tuple-element.15.z_ref, bf16[16384,1280]{1,0:T(8,128)(2,1)} %get-tuple-element.16.e_ref, bf16[2048,1280]{1,0:T(8,128)(2,1)} %h_ref.3, f32[1,1280]{1,0:T(1,128)} %reshape.48.gain_ref, ...), custom_call_target="tpu_custom_call" | custom-call | flops 85899345920 | bytes 134217728 | tf_op jit(solution)/shard_map/own_grad/pallas_call | solution.py:287
  317.4 0.1 all-gather.8.cloned.1.call-update
  317.4 0.1 all-gather.12.cloned.1.call-start
  317.5 0.7 all-gather.12.cloned.1.call-update
  318.2 0.1 all-gather.14.cloned.1.call-start
  318.3 0.6 all-gather.14.cloned.1.call-update
  318.9 0.2 all-gather.10.cloned.1.call-start
  319.1 0.4 all-gather.10.cloned.1.call-update
  319.5 1.4 slice.19
  320.9 17.3 %all-gather.8.cloned.1.call-done = f32[256,1280]{1,0:T(8,128)} async-done(((f32[32,1280]{1,0:T(8,128)}), f32[256,1280]{1,0:T(8,128)}) %all-gather.8.cloned.1.call-update) | async-done | bytes 1310736 | tf_op jit(solution)/shard_map/all_gather | solution.py:386
  338.2 1.0 slice_reduce_fusion
  339.2 0.6 slice_reduce_fusion.3
  341.1 0.6 slice_reduce_fusion.1
  341.8 17.4 %all-gather.12.cloned.1.call-done.lse_ref = f32[128,2048]{1,0:T(8,128)} async-done(((f32[16,2048]{1,0:T(8,128)}), f32[128,2048]{1,0:T(8,128)}) %all-gather.12.cloned.1.call-update) | async-done | bytes 1048592 | tf_op jit(solution)/shard_map/all_gather | solution.py:379
  359.1 99.7 %all-gather.14.cloned.1.call-done.x_ref = bf16[8192,1280]{1,0:T(8,128)(2,1)} async-done(((bf16[1024,1280]{1,0:T(8,128)(2,1)}), bf16[8192,1280]{1,0:T(8,128)(2,1)}) %all-gather.14.cloned.1.call-update) | async-done | bytes 20971536 | tf_op jit(solution)/shard_map/all_gather | solution.py:378
  458.9 99.1 %d_embed.2.refs_0_ = f32[2048,1280]{1,0:T(8,128)} custom-call(s32[1]{0:T(128)} %bitcast.38.first_ref, f32[1]{0:T(128)} %bitcast.39.count_ref, bf16[8192,1280]{1,0:T(8,128)(2,1)} %all-gather.14.cloned.1.call-done.x_ref, bf16[2048,1280]{1,0:T(8,128)(2,1)} %e_ref.3, f32[128,2048]{1,0:T(8,128)} %all-gather.12.cloned.1.call-done.lse_ref, ...), custom_call_target="tpu_custom_call" | custom-call | flops 85899345920 | bytes 41943040 | tf_op jit(solution)/shard_map/d_embed/pallas_call | solution.py:351
  557.9 1.6 all-gather.10.cloned.1.call-done.x_ref
  559.5 103.0 %d_embed.3 = f32[2048,1280]{1,0:T(8,128)} custom-call(s32[1]{0:T(128)} %bitcast.38.first_ref, f32[1]{0:T(128)} %bitcast.39.count_ref, bf16[8192,1280]{1,0:T(8,128)(2,1)} %all-gather.10.cloned.1.call-done.x_ref, bf16[2048,1280]{1,0:T(8,128)(2,1)} %e_ref.3, f32[128,2048]{1,0:T(8,128)} %all-gather.12.cloned.1.call-done.lse_ref, ...), custom_call_target="tpu_custom_call" | custom-call | flops 85899345920 | bytes 41943040 | tf_op jit(solution)/shard_map/d_embed/pallas_call | solution.py:351
Async XLA Ops:
  7.2 183.7 %all-gather.6.cloned.1.call-start = ((), (), s32[]{:S(2)}) async-start(), calls=%async_computation | async-start | bytes 1179648 | tf_op jit(solution)/shard_map/all_gather | solution.py:371
  8.7 329.5 %all-gather.8.cloned.1.call-start = ((), (), s32[]{:S(2)}) async-start(), calls=%async_computation.1 | async-start | bytes 1474560 | tf_op jit(solution)/shard_map/all_gather | solution.py:386
  11.4 181.3 %copy-start = (s32[2048]{0:T(1024)S(1)}, s32[2048]{0:T(1024)}, u32[]{:S(2)}) copy-start(s32[2048]{0:T(1024)} %param.11) | copy-start | bytes 24580
  317.4 41.7 %all-gather.12.cloned.1.call-start = ((), (), s32[]{:S(2)}) async-start(), calls=%async_computation.3 | async-start | bytes 1179648 | tf_op jit(solution)/shard_map/all_gather | solution.py:379
  318.2 140.6 %all-gather.14.cloned.1.call-start = ((), (), s32[]{:S(2)}) async-start(), calls=%async_computation.4 | async-start | bytes 23592960 | tf_op jit(solution)/shard_map/all_gather | solution.py:378
  318.9 240.7 %all-gather.10.cloned.1.call-start = ((), (), s32[]{:S(2)}) async-start(), calls=%async_computation.2 | async-start | bytes 23592960 | tf_op jit(solution)/shard_map/all_gather | solution.py:378
Sparse Core Ops, SparseCore 0:
  10.2 23.6 all-gather.5
  317.5 20.6 all-gather.7
  339.8 19.2 all-gather.11
  360.5 98.2 all-gather.13
  460.3 99.2 all-gather.9

commit v2 on v1

--- a/solution.py
+++ b/solution.py
@@ -30,7 +30,8 @@
 FOREIGN = [(NEAR, 0), (FAR, 0), (NEAR, 1), (FAR, 1), (FAR, 2), (NEAR, 2), (OPPOSITE, 0), (FAR, 3), (NEAR, 3), (OPPOSITE, 1), (OPPOSITE, 2), (OPPOSITE, 3)]
 LINK = {item: item[1] for item in FOREIGN if item[0] == NEAR}
 LINK.update({(FAR, 0): 4, (FAR, 1): 5, (OPPOSITE, 0): 6, (OPPOSITE, 1): 7, (FAR, 2): 8, (FAR, 3): 9, (OPPOSITE, 2): 10, (OPPOSITE, 3): 11})
-SIBLING = 12
+SPLIT = {'ahead': 12, 'back': 13, 'across': LINK[OPPOSITE, 3]}
+SIBLING = 14
 COPIES = SIBLING + PIECES + len(FOREIGN)
 CHIPS = 4
 
@@ -59,7 +60,7 @@
 
 def logits_body(rows, h_ref, gain_ref, bias_ref, own_ref, *refs):
     x_refs = refs[:TOKEN_CHUNKS]
-    lse_ref, norms_ref, all_ref, z_ref, e_buf, z_buf, m_ref, s_ref, e_sem, o_sem, z_sem, send_sem, recv_sem = refs[TOKEN_CHUNKS:]
+    lse_ref, norms_ref, all_ref, z_ref, zt_ref, e_buf, z_buf, t_buf, m_ref, s_ref, e_sem, o_sem, z_sem, t_sem, send_sem, recv_sem = refs[TOKEN_CHUNKS:]
     i = pl.program_id(0)
     steps = len(ORDER)
     tile = e_buf.shape[1]
@@ -76,20 +77,26 @@
         'across': (dp + sign, me),
     }
 
-    def rows_of(entry):
+    third = tile // 3 // 16 * 16 + 16
+    shares = {'ahead': (0, third), 'back': (third, third), 'across': (2 * third, tile - 2 * third)}
+
+    def rows_of(entry, share=None):
         shard, piece = place(*entry)
-        return pl.ds(pl.multiple_of(shard * shard_rows + piece * tile, tile), tile)
+        begin, size = shares[share] if share else (0, tile)
+        return pl.ds(pl.multiple_of(shard * shard_rows + piece * tile + begin, 16), size)
 
     def own_rows(n):
         return pl.ds(pl.multiple_of(place(0, 0, n)[1] * tile, tile), tile)
 
-    def remote(to, number, entry, own=False):
-        at = rows_of(entry)
+    def remote(to, number, entry, own=False, share=None):
+        at = rows_of(entry, share)
         source = own_ref.at[own_rows(entry[2]), :] if own else all_ref.at[at, :]
         return pltpu.make_async_remote_copy(source, all_ref.at[at, :], send_sem.at[number], recv_sem.at[number], device_id=targets[to], device_id_type=pl.DeviceIdType.MESH)
 
-    def arrived(number):
-        remote('sibling', number, ORDER[0]).wait_recv()
+    numbers = [(number, None) for number in range(COPIES) if number not in SPLIT.values()] + [(SPLIT[share], share) for share in SPLIT]
+
+    def arrived(number, share=None):
+        remote('sibling', number, ORDER[0], share=share).wait_recv()
 
     def load(step):
         entry = ORDER[step]
@@ -110,7 +117,11 @@
         if core_of == 1:
             arrived(SIBLING + PIECES + number)
             return
-        arrived(LINK[chip_of, n])
+        if (chip_of, n) == (OPPOSITE, 3):
+            for share in SPLIT:
+                arrived(SPLIT[share], share)
+        else:
+            arrived(LINK[chip_of, n])
         entry = ORDER[step]
         remote('sibling', SIBLING + PIECES + number, entry).start()
         if n < 2:
@@ -119,7 +130,11 @@
             elif chip_of == NEAR:
                 remote('across', LINK[FAR, n + 2], entry).start()
             else:
-                remote('across', LINK[OPPOSITE, n + 2], entry).start()
+                share = 'across' if n == 1 else None
+                remote('across', LINK[OPPOSITE, n + 2], entry, share=share).start()
+        elif n == 3 and chip_of != OPPOSITE:
+            share = 'ahead' if chip_of == NEAR else 'back'
+            remote(share, SPLIT[share], entry, share=share).start()
 
     @pl.when(i == 0)
     def _():
@@ -179,6 +194,19 @@
         s_ref[part, :] = total
     written(i).start()
 
+    def turned(step):
+        return pltpu.make_async_copy(t_buf, zt_ref.at[own_rows(step), :], t_sem)
+
+    @pl.when((i >= 1) & (i <= PIECES))
+    def _():
+        turned(i - 1).wait()
+
+    @pl.when(i < PIECES)
+    def _():
+        for r in range(0, h_ref.shape[0], rows):
+            t_buf[:, r:r + rows] = lax.dot_general(e_buf[slot], x_refs[r // held][r % held:r % held + rows, :], (((1,), (1,)), ((), ())), preferred_element_type=F32)
+        turned(i).start()
+
     @pl.when(i == steps - 1)
     def _():
         m = m_ref[...]
@@ -189,8 +217,8 @@
         norms_ref[...] = lse.T[:norms_ref.shape[0]]
         written(i - 1).wait()
         written(i).wait()
-        for number in range(COPIES):
-            remote('sibling', number, ORDER[0]).wait_send()
+        for number, share in numbers:
+            remote('sibling', number, ORDER[0], share=share).wait_send()
 
 
 def logits_call(hidden, gain, bias, embed, vocab, copies, rows=256):
@@ -199,35 +227,39 @@
     whole = lambda shape: pl.BlockSpec(shape, lambda i: (0, 0), pipeline_mode=pl.Buffered(1))
     fixed = lambda shape: pl.BlockSpec(shape, lambda i: (0, 0))
     hbm = pl.BlockSpec(memory_space=pl.ANY)
+    line = pl.BlockSpec((dim,), lambda i: (0,))
     return pl.pallas_call(
         functools.partial(logits_body, rows),
         grid=(len(ORDER),),
-        in_specs=[whole((tokens, dim)), whole((1, dim)), whole((1, dim)), hbm],
-        out_specs=[fixed((tokens // TOKEN_CHUNKS, dim))] * TOKEN_CHUNKS + [fixed((tokens, LANES)), fixed((copies, tokens)), hbm, hbm],
+        in_specs=[whole((tokens, dim)), line, line, hbm],
+        out_specs=[fixed((tokens // TOKEN_CHUNKS, dim))] * TOKEN_CHUNKS + [fixed((tokens, LANES)), fixed((copies, tokens)), hbm, hbm, hbm],
         out_shape=[jax.ShapeDtypeStruct((tokens // TOKEN_CHUNKS, dim), BF16)] * TOKEN_CHUNKS + [
             jax.ShapeDtypeStruct((tokens, LANES), F32),
             jax.ShapeDtypeStruct((copies, tokens), F32),
             jax.ShapeDtypeStruct((vocab, dim), BF16),
             jax.ShapeDtypeStruct((tokens, vocab), F32),
+            jax.ShapeDtypeStruct((embed.shape[0], tokens), F32),
         ],
         scratch_shapes=[
             pltpu.VMEM((2, tile, dim), BF16),
             pltpu.VMEM((2, tokens, tile), F32),
+            pltpu.VMEM((tile, tokens), F32),
             pltpu.VMEM((tokens, LANES), F32),
             pltpu.VMEM((tokens, LANES), F32),
             pltpu.SemaphoreType.DMA((2,)),
             pltpu.SemaphoreType.DMA((2,)),
             pltpu.SemaphoreType.DMA((2,)),
+            pltpu.SemaphoreType.DMA,
             pltpu.SemaphoreType.DMA((COPIES,)),
             pltpu.SemaphoreType.DMA((COPIES,)),
         ],
         compiler_params=pltpu.CompilerParams(vmem_limit_bytes=VMEM_LIMIT, dimension_semantics=('arbitrary',), collective_id=0, has_side_effects=True),
         cost_estimate=cost(1, tokens, vocab, dim, 4 * tokens * vocab),
         name='logits',
-    )(hidden, gain.reshape(1, dim), bias.reshape(1, dim), embed)
-
-
-def own_grad_body(rows, order_ref, z_ref, e_ref, h_ref, gain_ref, lse_ref, tgt_row, w_row, dh_ref, loss_ref, sums_ref, acc_ref, t_ref, tgt_ref, w_ref):
+    )(hidden, gain, bias, embed)
+
+
+def own_grad_body(rows, repeats, order_ref, z_ref, e_ref, h_ref, gain_ref, lse_ref, info_ref, dh_ref, loss_ref, sums_ref, count_ref, acc_ref, t_ref, tgt_ref, w_ref):
     i = pl.program_id(0)
     tokens, tile = z_ref.shape
     base = order_ref[i] * tile
@@ -236,8 +268,11 @@
     def _():
         acc_ref[...] = jnp.zeros_like(acc_ref)
         t_ref[...] = jnp.zeros_like(t_ref)
-        tgt_ref[...] = jnp.broadcast_to(tgt_row[...], (LANES, tokens)).T
-        w_ref[...] = jnp.broadcast_to(w_row[...], (LANES, tokens)).T
+        total = jnp.sum((info_ref[...] & 1).astype(F32)) / repeats
+        count_ref[...] = jnp.full_like(count_ref, total)
+        own = info_ref[pl.ds(pl.multiple_of(lax.axis_index('tp') * repeats, repeats), 1), :]
+        tgt_ref[...] = jnp.broadcast_to(own >> 1, (LANES, tokens)).T
+        w_ref[...] = jnp.broadcast_to((own & 1).astype(F32) / count_ref[0:1, 0:1], (LANES, tokens)).T
 
     lane = lax.broadcasted_iota(jnp.int32, (rows, LANES), 1)
     for r in range(0, tokens, rows):
@@ -279,13 +314,13 @@
             dh_ref[part, :] = (inv_std * (g - centre_term - x_hat * proj_term)).astype(BF16)
 
 
-def own_grad_call(order, z, e, hidden, gain, lse, tgt, w, tile, copies, rows=256):
+def own_grad_call(order, z, e, hidden, gain, lse, info, tile, copies, rows=256):
     tokens, vocab = z.shape
     dim = e.shape[1]
     once = lambda shape: pl.BlockSpec(shape, lambda i, order: (0, 0), pipeline_mode=pl.Buffered(1))
     fixed = lambda shape: pl.BlockSpec(shape, lambda i, order: (0, 0))
     return pl.pallas_call(
-        functools.partial(own_grad_body, rows),
+        functools.partial(own_grad_body, rows, info.shape[0] * tokens // vocab),
         grid_spec=pltpu.PrefetchScalarGridSpec(
             num_scalar_prefetch=1,
             grid=(vocab // tile,),
@@ -293,12 +328,11 @@
                 pl.BlockSpec((tokens, tile), lambda i, order: (0, i)),
                 pl.BlockSpec((tile, dim), lambda i, order: (order[i], 0)),
                 once((tokens, dim)),
-                once((1, dim)),
+                pl.BlockSpec((dim,), lambda i, order: (0,)),
                 once((tokens, LANES)),
-                once((1, tokens)),
-                once((1, tokens)),
+                once(info.shape),
             ],
-            out_specs=[fixed((tokens, dim)), fixed((8, tokens)), fixed((copies, dim))],
+            out_specs=[fixed((tokens, dim)), fixed((8, tokens)), fixed((copies, dim)), fixed((8, LANES))],
             scratch_shapes=[
                 pltpu.VMEM((tokens, dim), F32),
                 pltpu.VMEM((tokens, LANES), F32),
@@ -310,54 +344,85 @@
             jax.ShapeDtypeStruct((tokens, dim), BF16),
             jax.ShapeDtypeStruct((8, tokens), F32),
             jax.ShapeDtypeStruct((copies, dim), F32),
+            jax.ShapeDtypeStruct((8, LANES), F32),
         ],
         compiler_params=params(),
         cost_estimate=cost(1, tokens, vocab, dim, 4 * tokens * vocab),
         name='own_grad',
-    )(order, z, e, hidden, gain.reshape(1, dim), lse, tgt, w)
-
-
-def d_embed_body(rows, first_ref, count_ref, x_ref, e_ref, lse_ref, info_ref, *refs):
-    o_ref = refs[-1]
-
-    @pl.when(pl.program_id(0) == 0)
-    def _():
-        if len(refs) == 1:
-            o_ref[...] = jnp.zeros_like(o_ref)
-        else:
-            pltpu.sync_copy(refs[0], o_ref)
-
-    width = x_ref.shape[0]
+    )(order, z, e, hidden, gain, lse, info)
+
+
+def d_embed_body(rows, chunk, rank_ref, x_ref, e_ref, lse_ref, info_ref, count_ref, zt_ref, *refs):
+    o_ref, z_buf, z_sem = refs[-3:] if len(refs) == 3 else refs[1:4]
+    i = pl.program_id(0)
+    last = pl.num_programs(0) - 1
+    shard, width = e_ref.shape[0], x_ref.shape[0]
+    fetches = [pltpu.make_async_copy(zt_ref.at[:, chunk * width:(chunk + 1) * width], z_buf, z_sem)]
+    if len(refs) > 3:
+        before_ref, before_buf, before_sem = refs[0], refs[4], refs[5]
+        fetches.append(pltpu.make_async_copy(before_ref, before_buf, before_sem))
+
+    @pl.when(i == 0)
+    def _():
+        for fetch in fetches:
+            fetch.start()
+        o_ref[...] = jnp.zeros_like(o_ref)
+
     info = info_ref[0:1, :]
-    lse, tgt, w = lse_ref[0:1, :], (info >> 1) - first_ref[0], (info & 1).astype(F32) / count_ref[0]
-    row = lax.broadcasted_iota(jnp.int32, (rows, width), 0)
-    for r in range(0, e_ref.shape[0], rows):
-        z = lax.dot_general(e_ref[r:r + rows, :], x_ref[...], (((1,), (1,)), ((), ())), preferred_element_type=F32)
+    lse, tgt, w = lse_ref[0:1, :], (info >> 1) - rank_ref[0] * shard, (info & 1).astype(F32) / count_ref[0:1, 0:1]
+
+    def part_of(r, z):
+        row = lax.broadcasted_iota(jnp.int32, (rows, width), 0)
         p = jnp.exp(z - lse)
         p = jnp.where(row == tgt - r, p - 1.0, p) * w
-        o_ref[r:r + rows, :] += jnp.dot(p.astype(BF16), x_ref[...], preferred_element_type=F32)
-
-
-def d_embed_call(first, count, x, e, lse, info, before, chunk, tile, rows=256):
+        return jnp.dot(p.astype(BF16), x_ref[...], preferred_element_type=F32)
+
+    @pl.when(i < last)
+    def _():
+        for r in range(0, shard, rows):
+            z = lax.dot_general(e_ref[r:r + rows, :], x_ref[...], (((1,), (1,)), ((), ())), preferred_element_type=F32)
+            o_ref[r:r + rows, :] += part_of(r, z)
+
+    @pl.when(i == last)
+    def _():
+        for fetch in fetches:
+            fetch.wait()
+        for r in range(0, shard, rows):
+            total = o_ref[r:r + rows, :] + part_of(r, z_buf[r:r + rows, :])
+            if len(fetches) > 1:
+                total = total + before_buf[r:r + rows, :]
+            o_ref[r:r + rows, :] = total
+
+
+def d_embed_call(rank, count, x, e, lse, info, zt, before, chunk, tile, rows=256):
     tokens, dim = x.shape
     shard = e.shape[0]
-    scalar = pl.BlockSpec(memory_space=pltpu.SMEM)
-    stat = lambda v: pl.BlockSpec((v.shape[0] * tile // tokens, tile), lambda i: (i, chunk))
-    in_specs = [scalar, scalar, pl.BlockSpec((tile, dim), lambda i: (i, 0)), pl.BlockSpec((shard, dim), lambda i: (0, 0)), stat(lse), stat(info)]
-    operands = [first.reshape(1), count.reshape(1), x, e, lse, info]
+    group = tokens // tile
+    whose = lambda i, rank: lax.rem(rank[0] + 1 + i, group)
+    stat = lambda v: pl.BlockSpec((v.shape[0] // group, tile), lambda i, rank: (whose(i, rank), chunk))
+    once = lambda shape: pl.BlockSpec(shape, lambda i, rank: (0, 0), pipeline_mode=pl.Buffered(1))
+    hbm = pl.BlockSpec(memory_space=pl.ANY)
+    in_specs = [pl.BlockSpec((tile, dim), lambda i, rank: (whose(i, rank), 0)), once((shard, dim)), stat(lse), stat(info), once(count.shape), hbm]
+    operands = [x, e, lse, info, count, zt]
+    scratch = [pltpu.VMEM((shard, tile), F32), pltpu.SemaphoreType.DMA]
     if before is not None:
-        in_specs.append(pl.BlockSpec(memory_space=pl.ANY))
+        in_specs.append(hbm)
         operands.append(before)
+        scratch += [pltpu.VMEM((shard, dim), F32), pltpu.SemaphoreType.DMA]
     return pl.pallas_call(
-        functools.partial(d_embed_body, rows),
-        grid=(tokens // tile,),
-        in_specs=in_specs,
-        out_specs=pl.BlockSpec((shard, dim), lambda i: (0, 0)),
+        functools.partial(d_embed_body, rows, chunk),
+        grid_spec=pltpu.PrefetchScalarGridSpec(
+            num_scalar_prefetch=1,
+            grid=(group,),
+            in_specs=in_specs,
+            out_specs=pl.BlockSpec((shard, dim), lambda i, rank: (0, 0)),
+            scratch_shapes=scratch,
+        ),
         out_shape=jax.ShapeDtypeStruct((shard, dim), F32),
         compiler_params=params(),
         cost_estimate=cost(2, tokens, shard, dim, 2 * tokens * dim + 8 * shard * dim),
         name='d_embed',
-    )(*operands)
+    )(rank.reshape(1), *operands)
 
 
 def solution(mesh):
@@ -369,10 +434,9 @@
         rank = lax.axis_index('tp')
         copies = lambda width: -(-MIN_GATHER // (4 * group * width))
         info = lax.all_gather(jnp.tile((targets * 2 + loss_mask).reshape(1, tokens), (copies(tokens), 1)), 'tp', tiled=True)
-        count = jnp.sum((info.reshape(group, -1, tokens)[:, 0] & 1).astype(F32))
 
         outs = logits_call(hidden, ln_gain, ln_bias, embed, shard * group, copies(tokens))
-        lse, norms, all_embed, z = outs[TOKEN_CHUNKS:]
+        lse, norms, all_embed, z, zt = outs[TOKEN_CHUNKS:]
         x_chunks = []
         for h in range(TOKEN_CHUNKS):
             x_chunks.append(lax.all_gather(outs[h], 'tp', tiled=True))
@@ -380,15 +444,14 @@
 
         places = [place(*entry) for entry in ORDER]
         order = jnp.stack([shard_of * PIECES + n for shard_of, n in places])
-        scale = loss_mask.astype(F32) / count
         extra = -(-copies(dim) // 8) * 8
-        d_hidden, loss, sums = own_grad_call(order, z, all_embed, hidden, ln_gain, lse, targets.reshape(1, tokens), scale.reshape(1, tokens), shard // PIECES, extra)
+        d_hidden, loss, sums, count = own_grad_call(order, z, all_embed, hidden, ln_gain, lse, info, shard // PIECES, extra)
         sums = jnp.sum(lax.all_gather(sums, 'tp', tiled=True).reshape(group, extra, dim)[:, :3], axis=0)
-        mean_loss = jnp.sum(sums[2, :LANES]) / LANES / count
+        mean_loss = sums[2, 0] / count[0, 0]
 
         d_embed = None
         for h in range(TOKEN_CHUNKS):
-            d_embed = d_embed_call(rank * shard, count, x_chunks[h], embed, norms, info, d_embed, h, tokens // TOKEN_CHUNKS)
+            d_embed = d_embed_call(rank, count, x_chunks[h], embed, norms, info, zt, d_embed, h, tokens // TOKEN_CHUNKS)
         return loss[0], mean_loss.reshape(1), d_hidden, d_embed, sums[0], sums[1]
 
     token_rows = P(('dp', 'tp'))

time: 671 us -> 645 us (0.961)
  Pallas kernels: 504 us -> 473 us
    pallas_call x1, Pallas kernels: 179 us -> 160 us  [logits_call(): pl.pallas_call(functools.partial(logits_body, rows), grid=(len(ORDER),),...]
    pallas_call x3, Pallas kernels: 326 us -> 312 us  [the longest x2 188 us: d_embed_call(): pl.pallas_call(functools.partial(d_embed_body, rows, chunk), grid_spec=pl...]
  transfers between devices with their start and end apart: 5 -> 5, of which waited for: 4 -> 4; matrix products, arithmetic and copies ran while one was open for 1% -> 1% of each run, Pallas kernels for 41% -> 40%
where the time goes in v2:
time: 645 us; the launch traced here: 638 us
  Pallas kernels  473 us (73%)
  waiting for transfers between devices  141 us (22%)
  between operations  16.8 us (3%)
    pallas_call x2, Pallas kernels, d_embed_call(): pl.pallas_call(functools.partial(d_embed_body, rows, chunk), grid_spec=pl...  188 us
    pallas_call x1, Pallas kernels, logits_call(): pl.pallas_call(functools.partial(logits_body, rows), grid=(len(ORDER),),...  160 us
    pallas_call x1, Pallas kernels, own_grad_call(): pl.pallas_call(functools.partial(own_grad_body, rows, info.shape[0] * tok...  124 us
    all_gather x2, waiting for transfers between devices, whole(): x_chunks.append(lax.all_gather(outs[h], 'tp', tiled=True))  107 us
    all_gather x1, waiting for transfers between devices, whole(): norms = lax.all_gather(norms, 'tp', tiled=True)  17.4 us
    all_gather x1, waiting for transfers between devices, whole(): lax.all_gather(sums, 'tp', tiled=True).reshape(group, extra, dim)[:, :3]  15.4 us
  transfers between devices with their start and end apart: 5, of which 4 were waited for; matrix products, arithmetic and copies ran while one was open for 1% of the time, Pallas kernels for 40%

profile of v2, /device:TPU:112, one launch (start us, length us, event | category | flops | bytes accessed | tf_op | source)
XLA Modules:
  0.0 638.0 jit_solution(11222034136425365700)
XLA Ops:
  7.2 0.1 all-gather.6.cloned.1.call-start
  7.2 0.7 multiply_add_fusion
  8.0 0.7 tile.2
  8.6 0.1 all-gather.6.cloned.1.call-update
  8.7 0.1 all-gather.8.cloned.1.call-start
  8.8 160.4 %logits.1 = (bf16[1024,1280]{1,0:T(8,128)(2,1)}, bf16[1024,1280]{1,0:T(8,128)(2,1)}, f32[2048,128]{1,0:T(8,128)}, f32[16,2048]{1,0:T(8,128)}, bf16[16384,1280]{1...) custom-call(bf16[2048,1280]{1,0:T(8,128)(2,1)} %h_ref.3, f32[1280]{0:T(1024)} %gain_ref.3, f32[1280]{0:T(1024)} %bias_ref.1, ...), custom_call_target="tpu_custom_call" | custom-call | flops 85899345920 | bytes 134217728 | tf_op jit(solution)/shard_map/logits/pallas_call | solution.py:231
  169.2 0.7 stack.131.order_ref
  169.9 0.0 all-gather.6.cloned.1.call-done.info_ref
  169.9 124.5 %own_grad.1 = (bf16[2048,1280]{1,0:T(8,128)(2,1)}, f32[8,2048]{1,0:T(8,128)}, f32[32,1280]{1,0:T(8,128)}, f32[8,128]{1,0:T(8,128)}) custom-call(s32[32]{0:T(128)} %stack.131.order_ref, f32[2048,16384]{1,0:T(8,128)} %get-tuple-element.17.z_ref, bf16[16384,1280]{1,0:T(8,128)(2,1)} %get-tuple-element.18.e_ref, bf16[2048,1280]{1,0:T(8,128)(2,1)} %h_ref.3, ...), custom_call_target="tpu_custom_call" | custom-call | flops 85899345920 | bytes 134217728 | tf_op jit(solution)/shard_map/own_grad/pallas_call | solution.py:322
  294.3 0.1 all-gather.8.cloned.1.call-update
  294.4 0.1 all-gather.12.cloned.1.call-start
  294.5 0.7 all-gather.12.cloned.1.call-update
  295.2 0.1 all-gather.14.cloned.1.call-start
  295.3 0.6 all-gather.14.cloned.1.call-update
  295.8 0.1 all-gather.10.cloned.1.call-start
  295.9 0.6 all-gather.10.cloned.1.call-update
  296.5 1.2 slice.21
  297.7 1.4 slice.18
  299.1 15.4 %all-gather.8.cloned.1.call-done = f32[256,1280]{1,0:T(8,128)} async-done(((f32[32,1280]{1,0:T(8,128)}), f32[256,1280]{1,0:T(8,128)}) %all-gather.8.cloned.1.call-update) | async-done | bytes 1310736 | tf_op jit(solution)/shard_map/all_gather | solution.py:449
  314.5 1.0 slice_reduce_fusion
  315.5 0.5 slice.25
  317.3 0.6 slice_reduce_fusion.1
  318.0 17.4 %all-gather.12.cloned.1.call-done.lse_ref = f32[128,2048]{1,0:T(8,128)} async-done(((f32[16,2048]{1,0:T(8,128)}), f32[128,2048]{1,0:T(8,128)}) %all-gather.12.cloned.1.call-update) | async-done | bytes 1048592 | tf_op jit(solution)/shard_map/all_gather | solution.py:443
  335.4 99.7 %all-gather.14.cloned.1.call-done.x_ref = bf16[8192,1280]{1,0:T(8,128)(2,1)} async-done(((bf16[1024,1280]{1,0:T(8,128)(2,1)}), bf16[8192,1280]{1,0:T(8,128)(2,1)}) %all-gather.14.cloned.1.call-update) | async-done | bytes 20971536 | tf_op jit(solution)/shard_map/all_gather | solution.py:442
  435.1 93.9 %d_embed.2.refs_0_ = f32[2048,1280]{1,0:T(8,128)} custom-call(s32[1]{0:T(128)} %bitcast.35.rank_ref, bf16[8192,1280]{1,0:T(8,128)(2,1)} %all-gather.14.cloned.1.call-done.x_ref, bf16[2048,1280]{1,0:T(8,128)(2,1)} %e_ref.3, f32[128,2048]{1,0:T(8,128)} %all-gather.12.cloned.1.call-done.lse_ref, s32[128,2048]{1,0:T(8,128)} %all-gather.6.cloned.1.call-done.info_ref, ...), custom_call_target="tpu_custom_call" | custom-call | flops 85899345920 | bytes 41943040 | tf_op jit(solution)/shard_map/d_embed/pallas_call | solution.py:412
  529.0 6.8 %all-gather.10.cloned.1.call-done.x_ref = bf16[8192,1280]{1,0:T(8,128)(2,1)} async-done(((bf16[1024,1280]{1,0:T(8,128)(2,1)}), bf16[8192,1280]{1,0:T(8,128)(2,1)}) %all-gather.10.cloned.1.call-update) | async-done | bytes 20971536 | tf_op jit(solution)/shard_map/all_gather | solution.py:442
  535.8 94.2 %d_embed.3 = f32[2048,1280]{1,0:T(8,128)} custom-call(s32[1]{0:T(128)} %bitcast.35.rank_ref, bf16[8192,1280]{1,0:T(8,128)(2,1)} %all-gather.10.cloned.1.call-done.x_ref, bf16[2048,1280]{1,0:T(8,128)(2,1)} %e_ref.3, f32[128,2048]{1,0:T(8,128)} %all-gather.12.cloned.1.call-done.lse_ref, s32[128,2048]{1,0:T(8,128)} %all-gather.6.cloned.1.call-done.info_ref, ...), custom_call_target="tpu_custom_call" | custom-call | flops 85899345920 | bytes 41943040 | tf_op jit(solution)/shard_map/d_embed/pallas_call | solution.py:412
Async XLA Ops:
  7.2 162.7 %all-gather.6.cloned.1.call-start = ((), (), s32[]{:S(2)}) async-start(), calls=%async_computation | async-start | bytes 1179648 | tf_op jit(solution)/shard_map/all_gather | solution.py:436
  8.7 305.8 %all-gather.8.cloned.1.call-start = ((), (), s32[]{:S(2)}) async-start(), calls=%async_computation.1 | async-start | bytes 1474560 | tf_op jit(solution)/shard_map/all_gather | solution.py:449
  294.4 41.0 %all-gather.12.cloned.1.call-start = ((), (), s32[]{:S(2)}) async-start(), calls=%async_computation.3 | async-start | bytes 1179648 | tf_op jit(solution)/shard_map/all_gather | solution.py:443
  295.2 139.9 %all-gather.14.cloned.1.call-start = ((), (), s32[]{:S(2)}) async-start(), calls=%async_computation.4 | async-start | bytes 23592960 | tf_op jit(solution)/shard_map/all_gather | solution.py:442
  295.8 240.0 %all-gather.10.cloned.1.call-start = ((), (), s32[]{:S(2)}) async-start(), calls=%async_computation.2 | async-start | bytes 23592960 | tf_op jit(solution)/shard_map/all_gather | solution.py:442
Sparse Core Ops, SparseCore 0:
  10.2 23.6 all-gather.5
  294.5 19.9 all-gather.7
  316.1 19.2 all-gather.11
  336.8 98.2 all-gather.13
  436.5 99.2 all-gather.9

commit v3 on v2

--- a/solution.py
+++ b/solution.py
@@ -179,19 +179,23 @@
         written(i - 2).wait()
 
     held = x_refs[0].shape[0]
-    for r in range(0, h_ref.shape[0], rows):
-        part = slice(r, r + rows)
-        z = lax.dot_general(x_refs[r // held][r % held:r % held + rows, :], e_buf[slot], (((1,), (1,)), ((), ())), preferred_element_type=F32)
-        z_buf[slot, part, :] = z
-        m_old = m_ref[part, :]
-        m_new = m_old
-        for g in range(0, tile, LANES):
-            m_new = jnp.maximum(m_new, z[:, g:g + LANES])
-        total = s_ref[part, :] * jnp.exp(m_old - m_new)
-        for g in range(0, tile, LANES):
-            total = total + jnp.exp(z[:, g:g + LANES] - m_new)
-        m_ref[part, :] = m_new
-        s_ref[part, :] = total
+    for c, x_ref in enumerate(x_refs):
+        @pl.loop(0, held // (2 * rows))
+        def _(a, c=c, x_ref=x_ref):
+            for b in range(2):
+                from_ = pl.multiple_of((2 * a + b) * rows, rows)
+                part = pl.ds(pl.multiple_of(c * held + from_, rows), rows)
+                z = lax.dot_general(x_ref[pl.ds(from_, rows), :], e_buf[slot], (((1,), (1,)), ((), ())), preferred_element_type=F32)
+                z_buf[slot, part, :] = z
+                m_old = m_ref[part, :]
+                m_new = m_old
+                for g in range(0, tile, LANES):
+                    m_new = jnp.maximum(m_new, z[:, g:g + LANES])
+                total = s_ref[part, :] * jnp.exp(m_old - m_new)
+                for g in range(0, tile, LANES):
+                    total = total + jnp.exp(z[:, g:g + LANES] - m_new)
+                m_ref[part, :] = m_new
+                s_ref[part, :] = total
     written(i).start()
 
     def turned(step):
@@ -203,8 +207,11 @@
 
     @pl.when(i < PIECES)
     def _():
-        for r in range(0, h_ref.shape[0], rows):
-            t_buf[:, r:r + rows] = lax.dot_general(e_buf[slot], x_refs[r // held][r % held:r % held + rows, :], (((1,), (1,)), ((), ())), preferred_element_type=F32)
+        for c, x_ref in enumerate(x_refs):
+            @pl.loop(0, tile // LANES)
+            def _(a, c=c, x_ref=x_ref):
+                part = pl.ds(pl.multiple_of(a * LANES, LANES), LANES)
+                t_buf[part, c * held:(c + 1) * held] = lax.dot_general(e_buf[slot, part, :], x_ref[...], (((1,), (1,)), ((), ())), preferred_element_type=F32)
         turned(i).start()
 
     @pl.when(i == steps - 1)
@@ -296,7 +303,7 @@
         loss = jnp.where(w_ref[...] > 0.0, loss, 0.0)
         loss_ref[...] = loss.T[:8]
         sums_ref[...] = jnp.zeros_like(sums_ref)
-        sums_ref[2:3, 0:LANES] = jnp.sum(loss, axis=0, keepdims=True)
+        sums_ref[2:3, 0:LANES] = jnp.sum(loss, axis=0, keepdims=True) / count_ref[0:1, :]
 
         @pl.loop(0, tokens // rows)
         def _(a):
@@ -387,11 +394,15 @@
     def _():
         for fetch in fetches:
             fetch.wait()
-        for r in range(0, shard, rows):
-            total = o_ref[r:r + rows, :] + part_of(r, z_buf[r:r + rows, :])
+
+        @pl.loop(0, shard // rows)
+        def _(a):
+            r = pl.multiple_of(a * rows, rows)
+            part = pl.ds(r, rows)
+            total = o_ref[part, :] + part_of(r, z_buf[part, :])
             if len(fetches) > 1:
-                total = total + before_buf[r:r + rows, :]
-            o_ref[r:r + rows, :] = total
+                total = total + before_buf[part, :]
+            o_ref[part, :] = total
 
 
 def d_embed_call(rank, count, x, e, lse, info, zt, before, chunk, tile, rows=256):
@@ -447,12 +458,11 @@
         extra = -(-copies(dim) // 8) * 8
         d_hidden, loss, sums, count = own_grad_call(order, z, all_embed, hidden, ln_gain, lse, info, shard // PIECES, extra)
         sums = jnp.sum(lax.all_gather(sums, 'tp', tiled=True).reshape(group, extra, dim)[:, :3], axis=0)
-        mean_loss = sums[2, 0] / count[0, 0]
 
         d_embed = None
         for h in range(TOKEN_CHUNKS):
             d_embed = d_embed_call(rank, count, x_chunks[h], embed, norms, info, zt, d_embed, h, tokens // TOKEN_CHUNKS)
-        return loss[0], mean_loss.reshape(1), d_hidden, d_embed, sums[0], sums[1]
+        return loss[0], sums[2, :1], d_hidden, d_embed, sums[0], sums[1]
 
     token_rows = P(('dp', 'tp'))
     token_mat = P(('dp', 'tp'), None)

time: 645 us -> 662 us (1.026)
  Pallas kernels: 473 us -> 501 us
    pallas_call x1, Pallas kernels: 160 us -> 184 us  [logits_call(): pl.pallas_call(functools.partial(logits_body, rows), grid=(len(ORDER),),...]
  transfers between devices with their start and end apart: 5 -> 5, of which waited for: 4 -> 4; matrix products, arithmetic and copies ran while one was open for 1% -> 1% of each run, Pallas kernels for 40% -> 42%
where the time goes in v3:
time: 662 us; the launch traced here: 661 us
  Pallas kernels  501 us (76%)
  waiting for transfers between devices  140 us (21%)
  between operations  14 us (2%)
    pallas_call x2, Pallas kernels, d_embed_call(): pl.pallas_call(functools.partial(d_embed_body, rows, chunk), grid_spec=pl...  192 us
    pallas_call x1, Pallas kernels, logits_call(): pl.pallas_call(functools.partial(logits_body, rows), grid=(len(ORDER),),...  184 us
    pallas_call x1, Pallas kernels, own_grad_call(): pl.pallas_call(functools.partial(own_grad_body, rows, info.shape[0] * tok...  124 us
    all_gather x2, waiting for transfers between devices, whole(): x_chunks.append(lax.all_gather(outs[h], 'tp', tiled=True))  104 us
    all_gather x1, waiting for transfers between devices, whole(): norms = lax.all_gather(norms, 'tp', tiled=True)  18.8 us
    all_gather x1, waiting for transfers between devices, whole(): lax.all_gather(sums, 'tp', tiled=True).reshape(group, extra, dim)[:, :3]  15.4 us
  transfers between devices with their start and end apart: 5, of which 4 were waited for; matrix products, arithmetic and copies ran while one was open for 1% of the time, Pallas kernels for 42%

profile of v3, /device:TPU:112, one launch (start us, length us, event | category | flops | bytes accessed | tf_op | source)
XLA Modules:
  0.0 661.2 jit_solution(12547913074933581037)
XLA Ops:
  7.2 0.1 all-gather.6.cloned.1.call-start
  7.2 0.7 multiply_add_fusion
  8.0 0.7 tile.2
  8.6 0.1 all-gather.6.cloned.1.call-update
  8.7 0.1 all-gather.8.cloned.1.call-start
  8.8 184.4 %logits.1 = (bf16[1024,1280]{1,0:T(8,128)(2,1)}, bf16[1024,1280]{1,0:T(8,128)(2,1)}, f32[2048,128]{1,0:T(8,128)}, f32[16,2048]{1,0:T(8,128)}, bf16[16384,1280]{1...) custom-call(bf16[2048,1280]{1,0:T(8,128)(2,1)} %h_ref.3, f32[1280]{0:T(1024)} %gain_ref.3, f32[1280]{0:T(1024)} %bias_ref.1, ...), custom_call_target="tpu_custom_call" | custom-call | flops 85899345920 | bytes 134217728 | tf_op jit(solution)/shard_map/logits/pallas_call | solution.py:238
  193.3 0.7 stack.131.order_ref
  194.0 0.0 all-gather.6.cloned.1.call-done.info_ref
  194.0 124.0 %own_grad.1 = (bf16[2048,1280]{1,0:T(8,128)(2,1)}, f32[8,2048]{1,0:T(8,128)}, f32[32,1280]{1,0:T(8,128)}, f32[8,128]{1,0:T(8,128)}) custom-call(s32[32]{0:T(128)} %stack.131.order_ref, f32[2048,16384]{1,0:T(8,128)} %get-tuple-element.17.z_ref, bf16[16384,1280]{1,0:T(8,128)(2,1)} %get-tuple-element.18.e_ref, bf16[2048,1280]{1,0:T(8,128)(2,1)} %h_ref.3, ...), custom_call_target="tpu_custom_call" | custom-call | flops 85899345920 | bytes 134217728 | tf_op jit(solution)/shard_map/own_grad/pallas_call | solution.py:329
  318.0 0.1 all-gather.8.cloned.1.call-update
  318.0 0.1 all-gather.12.cloned.1.call-start
  318.1 0.7 all-gather.12.cloned.1.call-update
  318.8 0.1 all-gather.14.cloned.1.call-start
  318.9 0.6 all-gather.14.cloned.1.call-update
  319.5 0.2 all-gather.10.cloned.1.call-start
  319.7 0.4 all-gather.10.cloned.1.call-update
  320.1 1.4 slice.15
  321.6 15.4 %all-gather.8.cloned.1.call-done = f32[256,1280]{1,0:T(8,128)} async-done(((f32[32,1280]{1,0:T(8,128)}), f32[256,1280]{1,0:T(8,128)}) %all-gather.8.cloned.1.call-update) | async-done | bytes 1310736 | tf_op jit(solution)/shard_map/all_gather | solution.py:460
  336.9 1.0 slice_reduce_fusion
  337.9 0.5 slice.21
  338.4 0.6 slice_reduce_fusion.1
  339.1 18.8 %all-gather.12.cloned.1.call-done.lse_ref = f32[128,2048]{1,0:T(8,128)} async-done(((f32[16,2048]{1,0:T(8,128)}), f32[128,2048]{1,0:T(8,128)}) %all-gather.12.cloned.1.call-update) | async-done | bytes 1048592 | tf_op jit(solution)/shard_map/all_gather | solution.py:454
  357.8 99.7 %all-gather.14.cloned.1.call-done.x_ref = bf16[8192,1280]{1,0:T(8,128)(2,1)} async-done(((bf16[1024,1280]{1,0:T(8,128)(2,1)}), bf16[8192,1280]{1,0:T(8,128)(2,1)}) %all-gather.14.cloned.1.call-update) | async-done | bytes 20971536 | tf_op jit(solution)/shard_map/all_gather | solution.py:453
  457.6 96.0 %d_embed.2.refs_0_ = f32[2048,1280]{1,0:T(8,128)} custom-call(s32[1]{0:T(128)} %bitcast.35.rank_ref, bf16[8192,1280]{1,0:T(8,128)(2,1)} %all-gather.14.cloned.1.call-done.x_ref, bf16[2048,1280]{1,0:T(8,128)(2,1)} %e_ref.3, f32[128,2048]{1,0:T(8,128)} %all-gather.12.cloned.1.call-done.lse_ref, s32[128,2048]{1,0:T(8,128)} %all-gather.6.cloned.1.call-done.info_ref, ...), custom_call_target="tpu_custom_call" | custom-call | flops 85899345920 | bytes 41943040 | tf_op jit(solution)/shard_map/d_embed/pallas_call | solution.py:423
  553.6 4.7 all-gather.10.cloned.1.call-done.x_ref
  558.3 96.4 %d_embed.3 = f32[2048,1280]{1,0:T(8,128)} custom-call(s32[1]{0:T(128)} %bitcast.35.rank_ref, bf16[8192,1280]{1,0:T(8,128)(2,1)} %all-gather.10.cloned.1.call-done.x_ref, bf16[2048,1280]{1,0:T(8,128)(2,1)} %e_ref.3, f32[128,2048]{1,0:T(8,128)} %all-gather.12.cloned.1.call-done.lse_ref, s32[128,2048]{1,0:T(8,128)} %all-gather.6.cloned.1.call-done.info_ref, ...), custom_call_target="tpu_custom_call" | custom-call | flops 85899345920 | bytes 41943040 | tf_op jit(solution)/shard_map/d_embed/pallas_call | solution.py:423
Async XLA Ops:
  7.2 186.8 %all-gather.6.cloned.1.call-start = ((), (), s32[]{:S(2)}) async-start(), calls=%async_computation | async-start | bytes 1179648 | tf_op jit(solution)/shard_map/all_gather | solution.py:447
  8.7 328.2 %all-gather.8.cloned.1.call-start = ((), (), s32[]{:S(2)}) async-start(), calls=%async_computation.1 | async-start | bytes 1474560 | tf_op jit(solution)/shard_map/all_gather | solution.py:460
  318.0 39.8 %all-gather.12.cloned.1.call-start = ((), (), s32[]{:S(2)}) async-start(), calls=%async_computation.3 | async-start | bytes 1179648 | tf_op jit(solution)/shard_map/all_gather | solution.py:454
  318.8 138.7 %all-gather.14.cloned.1.call-start = ((), (), s32[]{:S(2)}) async-start(), calls=%async_computation.4 | async-start | bytes 23592960 | tf_op jit(solution)/shard_map/all_gather | solution.py:453
  319.5 238.8 %all-gather.10.cloned.1.call-start = ((), (), s32[]{:S(2)}) async-start(), calls=%async_computation.2 | async-start | bytes 23592960 | tf_op jit(solution)/shard_map/all_gather | solution.py:453
Sparse Core Ops, SparseCore 0:
  10.2 23.7 all-gather.5
  318.2 18.7 all-gather.7
  338.5 19.2 all-gather.11
  359.3 98.2 all-gather.13
  459.0 99.2 all-gather.9
